TPU v7x, 128 devices: a whole 4x4x4 slice. The times are simulated.
128 devices in a mesh: ep: 4 (over z), fsdp: 32 (over y, x, core).
Axes of the slice: x: 4, y: 4, z: 4, core: 2. Of those that a mesh axis runs over, the one named last changes fastest.
Arguments:
- train_gate: float32 [64, 2048, 1408], P('ep', 'fsdp'), may hold values from -0.25 to 0.25
- train_up: float32 [64, 2048, 1408], P('ep', 'fsdp'), may hold values from -0.25 to 0.25
- train_down: float32 [64, 1408, 2048], P('ep', None, 'fsdp'), may hold values from -0.3125 to 0.3125
- router_weight: float32 [2048, 64], P('fsdp', 'ep'), may hold values from -0.125 to 0.125
- router_gain: float32 [2048], P('fsdp'), may hold values from 0.25 to 1.75
Outputs:
- ready_gate: bfloat16 [64, 2048, 1408], P('ep', None, 'fsdp')
- ready_up: bfloat16 [64, 2048, 1408], P('ep', None, 'fsdp')
- ready_down: bfloat16 [64, 1408, 2048], P('ep', 'fsdp')
- scale_gate: float32 [64, 1408], P('ep', 'fsdp')
- scale_up: float32 [64, 1408], P('ep', 'fsdp')
- scale_down: float32 [64, 1408], P('ep', 'fsdp')
- serve_router: bfloat16 [2048, 64], replicated
All inputs are finite; a program needn't handle non-finite values.
Results may differ from a plain program's by a relative error of at most 0.001.
Values may be sent and summed in bfloat16 or wider, within the bound.
A program may use at most 192 MiB of HBM per device.

v0:
```python
import functools

import jax
import jax.numpy as jnp
from jax import lax
from jax.experimental import pallas as pl
from jax.experimental.pallas import tpu as pltpu
from jax.sharding import PartitionSpec as P

MESH = pl.DeviceIdType.MESH
F32, BF16 = jnp.float32, jnp.bfloat16

NX, NY, NZ = 4, 4, 4
EXP, ROWS, COLS = 16, 64, 1408
HALF = EXP // 2
PIECE = COLS // 32
TILES = COLS // 128
OFFS = [(dx, dy) for dy in range(NY) for dx in range(NX) if (dx, dy) != (0, 0)]
GROUP = 512


def exchange(
    gate, up, down, rw, gain,
    out_g, out_u, out_d, sc_g, sc_u, sc_d, rout,
    xf, xo, psum, rsbuf, myscl, scal, scal_o, tr, sb, big, rhalf, rbuf,
    lsem, osem, dsem_s, dsem_r, rs_s, rs_r, ag_s, ag_r, fw_s, fw_r, bk_s, bk_r,
    rt_s, rt_r,
):
    srcs, outs, scs = (gate, up, down), (out_g, out_u, out_d), (sc_g, sc_u, sc_d)
    f = lax.axis_index("fsdp")
    z = lax.axis_index("ep")
    core = lax.rem(f, 2)
    chip = lax.div(f, 2)
    x, y = lax.rem(chip, NX), lax.div(chip, NX)

    def chip_at(dx, dy):
        return lax.rem(y + dy, NY) * NX + lax.rem(x + dx, NX)

    def local(m, e):
        return pltpu.make_async_copy(
            srcs[m].at[core * HALF + e], xf.at[m, e, core], lsem.at[m, e])

    def other(e):
        return pltpu.make_async_copy(
            srcs[0].at[(1 - core) * HALF + e], xo.at[e], osem.at[e])

    def send(src, dst, ss, rs, dev):
        pltpu.make_async_remote_copy(
            src_ref=src, dst_ref=dst, send_sem=ss, recv_sem=rs,
            device_id={"fsdp": dev}, device_id_type=MESH).start()

    def await_bytes(ref, sem):
        pltpu.make_async_copy(ref, ref, sem).wait()

    for e in range(HALF):
        local(0, e).start()
        other(e).start()
    for m in (1, 2):
        for e in range(HALF):
            local(m, e).start()

    bar = pltpu.get_barrier_semaphore()
    for c in range(2):
        for dx, dy in OFFS:
            pl.semaphore_signal(bar, inc=1, device_id={"fsdp": chip_at(dx, dy) * 2 + c}, device_id_type=MESH)
    pl.semaphore_signal(bar, inc=1, device_id={"fsdp": f + 1 - 2 * core}, device_id_type=MESH)
    for dz in range(1, NZ):
        pl.semaphore_signal(bar, inc=1, device_id={"ep": lax.rem(z + dz, NZ)}, device_id_type=MESH)
    pl.semaphore_wait(bar, 31 + NZ - 1)

    mate = f + 1 - 2 * core
    for m in range(3):
        for e in range(HALF):
            send(srcs[m].at[(1 - core) * HALF + e], xf.at[m, e, core], dsem_s.at[m, e], dsem_r.at[m, e], mate)

    for k in range(4):
        psum[k, :, TILES] = jnp.ones((HALF, 1, 128), F32)

    def total_rows(parts, row):
        s = None
        for p in parts:
            q = jnp.sum(p * p, axis=0, keepdims=True)
            s = q if s is None else s + q
        for t in range(TILES):
            psum[row[0], row[1], t] = s[:, t * 128:(t + 1) * 128]

    def sums0(e, carry):
        local(0, e).wait()
        total_rows([xf[0, e, core]], (0, e))
        other(e).wait()
        total_rows([xo[e]], (3, e))
        return carry

    def sums(m, e, carry):
        local(m, e).wait()
        await_bytes(xf.at[m, e, 0], dsem_r.at[m, e])
        total_rows([xf[m, e, 0], xf[m, e, 1]], (m, e))
        return carry

    BASE = (0, 31, 46)

    def part(k, c):
        return psum.at[k, lax.div(c, 2), pl.ds(6 * lax.rem(c, 2), 6)]

    def rs_send(m):
        for k, (dx, dy) in enumerate(OFFS):
            c = chip_at(dx, dy)
            send(part(m, c), rsbuf.at[BASE[m] + k], rs_s.at[m], rs_r.at[m], c * 2 + core)
            if m == 0:
                send(part(3, c), rsbuf.at[15 + k], rs_s.at[m], rs_r.at[m], c * 2 + 1 - core)
        if m == 0:
            send(part(3, chip), rsbuf.at[30], rs_s.at[m], rs_r.at[m], mate)

    def ag_send(m):
        n = 31 if m == 0 else 15
        mine = rsbuf.at[pl.ds(BASE[m], n)]
        await_bytes(mine, rs_r.at[m])
        s = psum[m, lax.div(chip, 2), pl.ds(6 * lax.rem(chip, 2), 6)]
        for k in range(n):
            s = s + rsbuf[BASE[m] + k]
        s = jnp.sqrt(s)
        myscl[m] = s
        spot = scal.at[m, lax.div(chip, 2), pl.ds(6 * lax.rem(chip, 2), 6)]
        for dx, dy in OFFS:
            send(myscl.at[m], spot, ag_s.at[m], ag_r.at[m], chip_at(dx, dy) * 2 + core)
        scal[m, lax.div(chip, 2), pl.ds(6 * lax.rem(chip, 2), 6)] = s

    def ag_wait(m):
        await_bytes(rsbuf.at[pl.ds(0, 15)], ag_r.at[m])
        send(scal.at[m], scal_o.at[m], fw_s.at[m], fw_r.at[m], mate)

    def bulk(m, dy):
        row = lax.rem(y + dy, NY)
        first = jnp.minimum(lax.div(row * 352, 128), TILES - 4)
        slot = (m * 4 + dy) * GROUP

        def one(t, carry):
            tile = first + t
            lanes = pl.ds(pl.multiple_of(tile * 128, 128), 128)
            for e in range(HALF):
                inv = 1.0 / scal[m, e, tile]
                blk = jnp.concatenate([xf[m, e, 0, :, lanes], xf[m, e, 1, :, lanes]], axis=0)
                tr[pl.ds(e, 128, stride=8), :] = (blk * inv).T
            v = tr[...].reshape(128, 8, 128).astype(BF16)
            sb[pl.ds(slot + t * 128, 128)] = v
            return carry

        lax.fori_loop(0, 4, one, 0)
        for dx in (1, 3, 2, 0):
            for c in range(2):
                to = (row * NX + lax.rem(x + dx, NX)) * 2
                if dx == 0 and dy == 0:
                    if c == 1:
                        continue
                    to = mate
                else:
                    to = to + c
                at = slot + to * PIECE - first * 128
                send(
                    sb.at[pl.ds(at, PIECE)],
                    outs[m].at[:, pl.ds(pl.multiple_of(core * 8, 8), 8), pl.ds(pl.multiple_of(chip * 128, 128), 128)],
                    bk_s.at[m], bk_r.at[m], to)
        if dy == 0:
            at = slot + f * PIECE - first * 128
            lanes = pl.ds(pl.multiple_of(chip * 128, 128), 128)
            for c in range(2):
                @pl.when(core == c)
                def _():
                    def put(j, carry):
                        outs[m][j, 8 * c:8 * c + 8, lanes] = sb[at + j]
                        return carry
                    lax.fori_loop(0, PIECE, put, 0)

    def route_pair():
        v = rw[...] * gain[...]
        rhalf[0] = jnp.concatenate([v, v], axis=1)
        send(rhalf.at[0], rhalf.at[1], rt_s.at[0], rt_r.at[0], mate)

    def route_plane():
        await_bytes(rhalf.at[1], rt_r.at[0])
        low = lax.broadcasted_iota(jnp.int32, (EXP, 128), 1) < 64
        mine = low == (core == 0)
        rbuf[z, chip] = jnp.where(mine, rhalf[0], rhalf[1]).astype(BF16)
        for dx, dy in OFFS:
            send(rbuf.at[z, chip], rbuf.at[z, chip], rt_s.at[1], rt_r.at[1], chip_at(dx, dy) * 2 + core)

    def route_line():
        await_bytes(rbuf.at[0, pl.ds(0, 15)], rt_r.at[1])
        for dz in range(1, NZ):
            pltpu.make_async_remote_copy(
                src_ref=rbuf.at[z], dst_ref=rbuf.at[z], send_sem=rt_s.at[2], recv_sem=rt_r.at[2],
                device_id={"ep": lax.rem(z + dz, NZ)}, device_id_type=MESH).start()

    def route_out():
        await_bytes(rbuf.at[pl.ds(0, 3)], rt_r.at[2])
        for a in range(NZ):
            for c in range(16):
                rout[a * EXP:(a + 1) * EXP, c * 128:(c + 1) * 128] = rbuf[a, c]

    def scale_out(m):
        await_bytes(scal_o.at[m], fw_r.at[m])
        for e in range(HALF):
            for t in range(TILES + 1):
                own, oth = scal[m, e, t], scal_o[m, e, t]
                big[e:e + 1, t * 128:(t + 1) * 128] = jnp.where(core == 0, own, oth)
                big[HALF + e:HALF + e + 1, t * 128:(t + 1) * 128] = jnp.where(core == 0, oth, own)
        start = f * PIECE
        t0, r = lax.div(start, 128), lax.rem(start, 128)
        a = big[:, pl.ds(pl.multiple_of(t0 * 128, 128), 128)]
        b = big[:, pl.ds(pl.multiple_of(t0 * 128 + 128, 128), 128)]
        shift = lax.rem(128 - r, 128)
        a, b = pltpu.roll(a, shift, 1), pltpu.roll(b, shift, 1)
        lane = lax.broadcasted_iota(jnp.int32, (EXP, 128), 1)
        scs[m][...] = jnp.where(lane < 128 - r, a, b)[:, :PIECE]

    route_pair()
    lax.fori_loop(0, HALF, sums0, 0)
    rs_send(0)
    route_plane()
    ag_send(0)
    lax.fori_loop(0, HALF, functools.partial(sums, 1), 0)
    rs_send(1)
    lax.fori_loop(0, HALF, lambda e, carry: (await_bytes(xf.at[0, e, 0], dsem_r.at[0, e]), carry)[1], 0)
    ag_wait(0)
    bulk(0, 1)
    ag_send(1)
    lax.fori_loop(0, HALF, functools.partial(sums, 2), 0)
    rs_send(2)
    bulk(0, 3)
    route_line()
    bulk(0, 2)
    bulk(0, 0)
    ag_send(2)
    ag_wait(1)
    for dy in (1, 3, 2, 0):
        bulk(1, dy)
    ag_wait(2)
    for dy in (1, 3, 2, 0):
        bulk(2, dy)
    for m in range(3):
        scale_out(m)
    route_out()

    for m in range(3):
        for e in range(HALF):
            await_bytes(xf.at[m, e, 0], dsem_s.at[m, e])
        await_bytes(rsbuf.at[pl.ds(0, 31 if m == 0 else 15)], rs_s.at[m])
        await_bytes(rsbuf.at[pl.ds(0, 15)], ag_s.at[m])
        await_bytes(scal.at[m], fw_s.at[m])
    await_bytes(rhalf.at[0], rt_s.at[0])
    await_bytes(rbuf.at[0, pl.ds(0, 15)], rt_s.at[1])
    await_bytes(rbuf.at[pl.ds(0, 3)], rt_s.at[2])
    for m in range(3):
        await_bytes(sb.at[pl.ds(0, 31 * PIECE)], bk_s.at[m])
        await_bytes(sb.at[pl.ds(0, 31 * PIECE)], bk_r.at[m])


def settle(*refs):
    n = len(refs) // 2
    sem = refs[-1]
    for i in range(n):
        pltpu.make_async_copy(refs[i], refs[n + i], sem.at[i]).start()
    for i in range(n):
        pltpu.make_async_copy(refs[i], refs[n + i], sem.at[i]).wait()


def body(train_gate, train_up, train_down, router_weight, router_gain):
    down = jnp.transpose(train_down, (0, 2, 1))
    shapes = (
        [jax.ShapeDtypeStruct((PIECE, EXP, 2048), BF16)] * 3
        + [jax.ShapeDtypeStruct((EXP, PIECE), F32)] * 3
        + [jax.ShapeDtypeStruct((EXP * NZ, 2048), BF16)]
    )
    vmem = pl.BlockSpec(memory_space=pltpu.VMEM)
    hbm = pl.BlockSpec(memory_space=pl.ANY)
    dma = pltpu.SemaphoreType.DMA
    got = pl.pallas_call(
        exchange,
        out_shape=shapes,
        in_specs=[hbm, hbm, hbm, vmem, vmem],
        out_specs=[vmem] * 7,
        scratch_shapes=[
            pltpu.VMEM((3, HALF, 2, ROWS, COLS), F32),
            pltpu.VMEM((HALF, ROWS, COLS), F32),
            pltpu.VMEM((4, HALF, TILES + 1, 1, 128), F32),
            pltpu.VMEM((61, 6, 1, 128), F32),
            pltpu.VMEM((3, 6, 1, 128), F32),
            pltpu.VMEM((3, HALF, TILES + 1, 1, 128), F32),
            pltpu.VMEM((3, HALF, TILES + 1, 1, 128), F32),
            pltpu.VMEM((1024, 128), F32),
            pltpu.VMEM((12 * GROUP, 8, 128), BF16),
            pltpu.VMEM((EXP, (TILES + 1) * 128), F32),
            pltpu.VMEM((2, EXP, 128), F32),
            pltpu.VMEM((NZ, 16, EXP, 128), BF16),
            dma((3, HALF)), dma((HALF,)), dma((3, HALF)), dma((3, HALF)),
            dma((3,)), dma((3,)), dma((3,)), dma((3,)), dma((3,)), dma((3,)), dma((3,)), dma((3,)),
            dma((3,)), dma((3,)),
        ],
        compiler_params=pltpu.CompilerParams(
            collective_id=0, has_side_effects=True, vmem_limit_bytes=44 * 1024 * 1024
        ),
        name="exchange",
    )(train_gate, train_up, down, router_weight.T, router_gain[None, :])
    done = pl.pallas_call(
        settle,
        out_shape=shapes,
        in_specs=[vmem] * 7,
        out_specs=[hbm] * 7,
        scratch_shapes=[dma((7,))],
        compiler_params=pltpu.CompilerParams(vmem_limit_bytes=2 * 1024 * 1024),
        name="settle",
    )(*got)
    g, u, d, sg, su, sd, r = done
    back = lambda a: jnp.transpose(a, (1, 2, 0))
    return back(g), back(u), jnp.transpose(d, (1, 0, 2)), sg, su, sd, r.T


def solution(mesh):
    return jax.shard_map(
        body,
        mesh=mesh,
        in_specs=(
            P("ep", "fsdp", None),
            P("ep", "fsdp", None),
            P("ep", None, "fsdp"),
            P("fsdp", "ep"),
            P("fsdp"),
        ),
        out_specs=(
            P("ep", None, "fsdp"),
            P("ep", None, "fsdp"),
            P("ep", "fsdp", None),
            P("ep", "fsdp"),
            P("ep", "fsdp"),
            P("ep", "fsdp"),
            P(),
        ),
        check_vma=False,
    )
```

profile of v0, /device:TPU:23, one launch (start us, length us, event | category | flops | bytes accessed | tf_op | source)
XLA Modules:
  0.0 156.8 jit_solution(2183723205097510406)
XLA Ops:
  0.6 0.0 copy-start
  0.6 0.7 copy-done
  1.3 0.0 copy-start.1
  1.3 0.7 copy-done.1
  2.0 151.3 %exchange.1 = (bf16[44,16,2048]{2,1,0:T(8,128)(2,1)S(1)}, bf16[44,16,2048]{2,1,0:T(8,128)(2,1)S(1)}, bf16[44,16,2048]{2,1,0:T(8,128)(2,1)S(1)}, f32[16,44]{1,0:T...) custom-call(f32[16,64,1408]{2,1,0:T(8,128)} %gate.1, f32[16,64,1408]{2,1,0:T(8,128)} %up.1, ...), custom_call_target="tpu_custom_call" | custom-call | tf_op jit(solution)/shard_map/exchange/pallas_call | solution.py:277
  153.3 3.5 %settle.1 = (bf16[44,16,2048]{2,1,0:T(8,128)(2,1)}, bf16[44,16,2048]{2,1,0:T(8,128)(2,1)}, bf16[44,16,2048]{2,1,0:T(8,128)(2,1)}, f32[16,44]{1,0:T(8,128)}, f32[...) custom-call(bf16[44,16,2048]{2,1,0:T(8,128)(2,1)S(1)} %get-tuple-element.21.refs_0_, ...), custom_call_target="tpu_custom_call" | custom-call | tf_op jit(solution)/shard_map/settle/pallas_call | solution.py:304
Async XLA Ops:
  0.6 0.7 copy-start
  1.3 0.7 copy-start.1
where the time goes:
time: 157 us
  Pallas kernels  155 us (99%)
    pallas_call x1, Pallas kernels, body(): pl.pallas_call(exchange, out_shape=shapes, in_specs=[hbm, hbm, hbm, vmem,...  151 us
    pallas_call x1, Pallas kernels, body(): pl.pallas_call(settle, out_shape=shapes, in_specs=[vmem] * 7, out_specs=[...  3.55 us

commit v1 on v0

v1 whole, which is shorter than its diff:
```python
import functools

import jax
import jax.numpy as jnp
from jax import lax
from jax.experimental import pallas as pl
from jax.experimental.pallas import tpu as pltpu
from jax.sharding import PartitionSpec as P

MESH = pl.DeviceIdType.MESH
F32, BF16 = jnp.float32, jnp.bfloat16

NX, NY, NZ = 4, 4, 4
EXP, ROWS, COLS = 16, 64, 1408
HALF = EXP // 2
PIECE = COLS // 32
TILES = COLS // 128
OFFS = sorted([(dx, dy) for dy in range(NY) for dx in range(NX) if (dx, dy) != (0, 0)], key=lambda p: -(min(p[0], 4 - p[0]) + min(p[1], 4 - p[1])))
CUT = 4


def exchange(
    gate, up, down, rw_h, gain_h,
    out_g, out_u, out_d, sc_g, sc_u, sc_d, rout,
    xf, xo, psum, rsbuf, myscl, scal, scal_o, tr, sb, big, rw, gain, rhalf, rbuf,
    isem, lsem, osem, dsem_s, dsem_r, rs_s, rs_r, ag_s, ag_r, fw_s, fw_r, bk_s, bk_r,
    rt_s, rt_r,
):
    srcs, outs, scs = (gate, up, down), (out_g, out_u, out_d), (sc_g, sc_u, sc_d)
    f = lax.axis_index("fsdp")
    z = lax.axis_index("ep")
    core = lax.rem(f, 2)
    chip = lax.div(f, 2)
    x, y = lax.rem(chip, NX), lax.div(chip, NX)

    def chip_at(dx, dy):
        return lax.rem(y + dy, NY) * NX + lax.rem(x + dx, NX)

    def local(m, e):
        return pltpu.make_async_copy(
            srcs[m].at[core * HALF + e], xf.at[m, e, core], lsem.at[m, e])

    def other(m, e):
        return pltpu.make_async_copy(
            srcs[m].at[(1 - core) * HALF + e], xo.at[m, e], osem.at[m, e])

    def send(src, dst, ss, rs, dev):
        pltpu.make_async_remote_copy(
            src_ref=src, dst_ref=dst, send_sem=ss, recv_sem=rs,
            device_id={"fsdp": dev}, device_id_type=MESH).start()

    def await_bytes(ref, sem):
        pltpu.make_async_copy(ref, ref, sem).wait()

    rin = (pltpu.make_async_copy(rw_h, rw, isem.at[0]), pltpu.make_async_copy(gain_h, gain, isem.at[1]))
    for e in range(HALF):
        local(0, e).start()
        other(0, e).start()
    for c in rin:
        c.start()
    for m in (1, 2):
        for e in range(HALF):
            local(m, e).start()
            other(m, e).start()

    bar = pltpu.get_barrier_semaphore()
    for c in range(2):
        for dx, dy in OFFS:
            pl.semaphore_signal(bar, inc=1, device_id={"fsdp": chip_at(dx, dy) * 2 + c}, device_id_type=MESH)
    pl.semaphore_signal(bar, inc=1, device_id={"fsdp": f + 1 - 2 * core}, device_id_type=MESH)
    for dz in range(1, NZ):
        pl.semaphore_signal(bar, inc=1, device_id={"ep": lax.rem(z + dz, NZ)}, device_id_type=MESH)

    mate = f + 1 - 2 * core

    def swap(m, es=range(HALF)):
        for e in es:
            send(xo.at[m, e], xf.at[m, e, core], dsem_s.at[m], dsem_r.at[m], mate)

    for k in range(6):
        psum[k, :, TILES] = jnp.ones((HALF, 1, 128), F32)

    def total_rows(p, k, e):
        s = jnp.sum(p * p, axis=0, keepdims=True)
        for t in range(TILES):
            psum[k, e, t] = s[:, t * 128:(t + 1) * 128]

    def sums(m, e, carry):
        local(m, e).wait()
        total_rows(xf[m, e, core], m, e)
        other(m, e).wait()
        total_rows(xo[m, e], 3 + m, e)
        return carry

    def part(k, c):
        return psum.at[k, lax.div(c, 2), pl.ds(6 * lax.rem(c, 2), 6)]

    def rs_send(m):
        for k, (dx, dy) in enumerate(OFFS):
            c = chip_at(dx, dy)
            send(part(m, c), rsbuf.at[m, k], rs_s.at[m], rs_r.at[m], c * 2 + core)
            send(part(3 + m, c), rsbuf.at[m, 15 + k], rs_s.at[m], rs_r.at[m], c * 2 + 1 - core)
        send(part(3 + m, chip), rsbuf.at[m, 30], rs_s.at[m], rs_r.at[m], mate)

    def ag_send(m):
        await_bytes(rsbuf.at[m], rs_r.at[m])
        s = psum[m, lax.div(chip, 2), pl.ds(6 * lax.rem(chip, 2), 6)]
        for k in range(31):
            s = s + rsbuf[m, k]
        s = jnp.sqrt(s)
        myscl[m] = s
        spot = scal.at[m, lax.div(chip, 2), pl.ds(6 * lax.rem(chip, 2), 6)]
        for dx, dy in OFFS:
            send(myscl.at[m], spot, ag_s.at[m], ag_r.at[m], chip_at(dx, dy) * 2 + core)
        scal[m, lax.div(chip, 2), pl.ds(6 * lax.rem(chip, 2), 6)] = s

    def ag_wait(m):
        await_bytes(rsbuf.at[0, pl.ds(0, 15)], ag_r.at[m])
        send(scal.at[m], scal_o.at[m], fw_s.at[m], fw_r.at[m], mate)

    def fill(m):
        def one(t, carry):
            lanes = pl.ds(pl.multiple_of(t * 128, 128), 128)
            for e in range(HALF):
                inv = 1.0 / scal[m, e, t]
                blk = jnp.concatenate([xf[m, e, 0, :, lanes], xf[m, e, 1, :, lanes]], axis=0)
                tr[pl.ds(e, 128, stride=8), :] = (blk * inv).T
            sb[m, pl.ds(t * 128, 128)] = tr[...].reshape(128, 8, 128).astype(BF16)
            return carry

        lax.fori_loop(0, TILES, one, 0)

    def bulk(m):
        n = PIECE // CUT

        def go(to, h):
            send(
                sb.at[m, pl.ds(to * PIECE + h * n, n)],
                outs[m].at[pl.ds(h * n, n), pl.ds(pl.multiple_of(core * 8, 8), 8), pl.ds(pl.multiple_of(chip * 128, 128), 128)],
                bk_s.at[m], bk_r.at[m], to)

        def turn(h, carry):
            for c in range(2):
                for dx, dy in OFFS:
                    go(chip_at(dx, dy) * 2 + (core if c == 0 else 1 - core), h)
            go(mate, h)
            return carry

        if m == 0:
            for h in range(CUT):
                turn(h, 0)
                swap(1 + h // 2, range(4 * (h % 2), 4 * (h % 2) + 4))
        else:
            lax.fori_loop(0, CUT, turn, 0)
        lanes = pl.ds(pl.multiple_of(chip * 128, 128), 128)
        for c in range(2):
            @pl.when(core == c)
            def _():
                def put(j, carry):
                    outs[m][j, 8 * c:8 * c + 8, lanes] = sb[m, f * PIECE + j]
                    return carry
                lax.fori_loop(0, PIECE, put, 0)

    def route_pair():
        for c in rin:
            c.wait()
        v = rw[...] * gain[...]
        rhalf[0] = jnp.concatenate([v, v], axis=1)
        send(rhalf.at[0], rhalf.at[1], rt_s.at[0], rt_r.at[0], mate)

    def route_plane():
        await_bytes(rhalf.at[1], rt_r.at[0])
        low = lax.broadcasted_iota(jnp.int32, (EXP, 128), 1) < 64
        mine = low == (core == 0)
        rbuf[z, chip] = jnp.where(mine, rhalf[0], rhalf[1]).astype(BF16)
        for dx, dy in OFFS:
            send(rbuf.at[z, chip], rbuf.at[z, chip], rt_s.at[1], rt_r.at[1], chip_at(dx, dy) * 2 + core)

    def route_line():
        await_bytes(rbuf.at[0, pl.ds(0, 15)], rt_r.at[1])
        for dz in range(1, NZ):
            pltpu.make_async_remote_copy(
                src_ref=rbuf.at[z], dst_ref=rbuf.at[z], send_sem=rt_s.at[2], recv_sem=rt_r.at[2],
                device_id={"ep": lax.rem(z + dz, NZ)}, device_id_type=MESH).start()

    def route_out():
        await_bytes(rbuf.at[pl.ds(0, 3)], rt_r.at[2])
        for a in range(NZ):
            for c in range(16):
                rout[a * EXP:(a + 1) * EXP, c * 128:(c + 1) * 128] = rbuf[a, c]

    def scale_out(m):
        await_bytes(scal_o.at[m], fw_r.at[m])
        for e in range(HALF):
            for t in range(TILES + 1):
                own, oth = scal[m, e, t], scal_o[m, e, t]
                big[e:e + 1, t * 128:(t + 1) * 128] = jnp.where(core == 0, own, oth)
                big[HALF + e:HALF + e + 1, t * 128:(t + 1) * 128] = jnp.where(core == 0, oth, own)
        start = f * PIECE
        t0, r = lax.div(start, 128), lax.rem(start, 128)
        a = big[:, pl.ds(pl.multiple_of(t0 * 128, 128), 128)]
        b = big[:, pl.ds(pl.multiple_of(t0 * 128 + 128, 128), 128)]
        shift = lax.rem(128 - r, 128)
        a, b = pltpu.roll(a, shift, 1), pltpu.roll(b, shift, 1)
        lane = lax.broadcasted_iota(jnp.int32, (EXP, 128), 1)
        scs[m][...] = jnp.where(lane < 128 - r, a, b)[:, :PIECE]

    for m in range(3):
        lax.fori_loop(0, HALF, functools.partial(sums, m), 0)
        if m == 0:
            pl.semaphore_wait(bar, 31 + NZ - 1)
        rs_send(m)
        if m == 0:
            swap(0)
    route_pair()
    for m in range(3):
        ag_send(m)
    route_plane()
    for m in range(3):
        ag_wait(m)
        await_bytes(xo.at[m], dsem_r.at[m])
        fill(m)
        bulk(m)
    route_line()
    for m in range(3):
        scale_out(m)
    route_out()

    for m in range(3):
        await_bytes(xo.at[m], dsem_s.at[m])
        await_bytes(rsbuf.at[m], rs_s.at[m])
        await_bytes(rsbuf.at[0, pl.ds(0, 15)], ag_s.at[m])
        await_bytes(scal.at[m], fw_s.at[m])
    await_bytes(rhalf.at[0], rt_s.at[0])
    await_bytes(rbuf.at[0, pl.ds(0, 15)], rt_s.at[1])
    await_bytes(rbuf.at[pl.ds(0, 3)], rt_s.at[2])
    for m in range(3):
        await_bytes(sb.at[m, pl.ds(0, 31 * PIECE)], bk_s.at[m])
        await_bytes(sb.at[m, pl.ds(0, 31 * PIECE)], bk_r.at[m])


def settle(*refs):
    n = len(refs) // 2
    sem = refs[-1]
    for i in range(n):
        pltpu.make_async_copy(refs[i], refs[n + i], sem.at[i]).start()
    for i in range(n):
        pltpu.make_async_copy(refs[i], refs[n + i], sem.at[i]).wait()


def body(train_gate, train_up, train_down, router_weight, router_gain):
    down = jnp.transpose(train_down, (0, 2, 1))
    shapes = (
        [jax.ShapeDtypeStruct((PIECE, EXP, 2048), BF16)] * 3
        + [jax.ShapeDtypeStruct((EXP, PIECE), F32)] * 3
        + [jax.ShapeDtypeStruct((EXP * NZ, 2048), BF16)]
    )
    vmem = pl.BlockSpec(memory_space=pltpu.VMEM)
    hbm = pl.BlockSpec(memory_space=pl.ANY)
    dma = pltpu.SemaphoreType.DMA
    got = pl.pallas_call(
        exchange,
        out_shape=shapes,
        in_specs=[hbm] * 5,
        out_specs=[vmem] * 7,
        scratch_shapes=[
            pltpu.VMEM((3, HALF, 2, ROWS, COLS), F32),
            pltpu.VMEM((3, HALF, ROWS, COLS), F32),
            pltpu.VMEM((6, HALF, TILES + 1, 1, 128), F32),
            pltpu.VMEM((3, 31, 6, 1, 128), F32),
            pltpu.VMEM((3, 6, 1, 128), F32),
            pltpu.VMEM((3, HALF, TILES + 1, 1, 128), F32),
            pltpu.VMEM((3, HALF, TILES + 1, 1, 128), F32),
            pltpu.VMEM((1024, 128), F32),
            pltpu.VMEM((3, COLS, 8, 128), BF16),
            pltpu.VMEM((EXP, (TILES + 1) * 128), F32),
            pltpu.VMEM((EXP, ROWS), F32),
            pltpu.VMEM((1, ROWS), F32),
            pltpu.VMEM((2, EXP, 128), F32),
            pltpu.VMEM((NZ, 16, EXP, 128), BF16),
            dma((2,)), dma((3, HALF)), dma((3, HALF)), *[dma((3,))] * 12,
        ],
        compiler_params=pltpu.CompilerParams(
            collective_id=0, has_side_effects=True, vmem_limit_bytes=44 * 1024 * 1024
        ),
        name="exchange",
    )(train_gate, train_up, down, router_weight.T, router_gain[None, :])
    done = pl.pallas_call(
        settle,
        out_shape=shapes,
        in_specs=[vmem] * 7,
        out_specs=[hbm] * 7,
        scratch_shapes=[dma((7,))],
        compiler_params=pltpu.CompilerParams(vmem_limit_bytes=2 * 1024 * 1024),
        name="settle",
    )(*got)
    g, u, d, sg, su, sd, r = done
    back = lambda a: jnp.transpose(a, (1, 2, 0))
    return back(g), back(u), jnp.transpose(d, (1, 0, 2)), sg, su, sd, r.T


def solution(mesh):
    return jax.shard_map(
        body,
        mesh=mesh,
        in_specs=(
            P("ep", "fsdp", None),
            P("ep", "fsdp", None),
            P("ep", None, "fsdp"),
            P("fsdp", "ep"),
            P("fsdp"),
        ),
        out_specs=(
            P("ep", None, "fsdp"),
            P("ep", None, "fsdp"),
            P("ep", "fsdp", None),
            P("ep", "fsdp"),
            P("ep", "fsdp"),
            P("ep", "fsdp"),
            P(),
        ),
        check_vma=False,
    )
```

time: 157 us -> 121 us (0.77)
  the two profiles are of different devices: /device:TPU:23 before, /device:TPU:1 now
where the time goes in v1:
time: 121 us; the launch traced here: 120 us
  Pallas kernels  118 us (98%)
  local copies, waits for them, and re-layouts  1.34 us (1%)
    pallas_call x1, Pallas kernels, body(): pl.pallas_call(exchange, out_shape=shapes, in_specs=[hbm] * 5, out_specs=...  115 us
    pallas_call x1, Pallas kernels, body(): pl.pallas_call(settle, out_shape=shapes, in_specs=[vmem] * 7, out_specs=[...  3.55 us

profile of v1, /device:TPU:1, one launch (start us, length us, event | category | flops | bytes accessed | tf_op | source)
XLA Modules:
  0.0 120.5 jit_solution(8302226877308807269)
XLA Ops:
  0.6 0.0 copy-start
  0.6 0.7 copy-done
  1.3 0.0 copy-start.1
  1.3 0.7 copy-done.1
  2.0 114.9 %exchange.1 = (bf16[44,16,2048]{2,1,0:T(8,128)(2,1)S(1)}, bf16[44,16,2048]{2,1,0:T(8,128)(2,1)S(1)}, bf16[44,16,2048]{2,1,0:T(8,128)(2,1)S(1)}, f32[16,44]{1,0:T...) custom-call(f32[16,64,1408]{2,1,0:T(8,128)} %gate.1, f32[16,64,1408]{2,1,0:T(8,128)} %up.1, ...), custom_call_target="tpu_custom_call" | custom-call | tf_op jit(solution)/shard_map/exchange/pallas_call | solution.py:261
  116.9 3.5 %settle.1 = (bf16[44,16,2048]{2,1,0:T(8,128)(2,1)}, bf16[44,16,2048]{2,1,0:T(8,128)(2,1)}, bf16[44,16,2048]{2,1,0:T(8,128)(2,1)}, f32[16,44]{1,0:T(8,128)}, f32[...) custom-call(bf16[44,16,2048]{2,1,0:T(8,128)(2,1)S(1)} %get-tuple-element.21.refs_0_, ...), custom_call_target="tpu_custom_call" | custom-call | tf_op jit(solution)/shard_map/settle/pallas_call | solution.py:288
Async XLA Ops:
  0.6 0.7 copy-start
  1.3 0.7 copy-start.1

commit v2 on v1

--- a/solution.py
+++ b/solution.py
@@ -17,14 +17,15 @@
 TILES = COLS // 128
 OFFS = sorted([(dx, dy) for dy in range(NY) for dx in range(NX) if (dx, dy) != (0, 0)], key=lambda p: -(min(p[0], 4 - p[0]) + min(p[1], 4 - p[1])))
 CUT = 4
+RAW = 4
 
 
 def exchange(
     gate, up, down, rw_h, gain_h,
     out_g, out_u, out_d, sc_g, sc_u, sc_d, rout,
-    xf, xo, psum, rsbuf, myscl, scal, scal_o, tr, sb, big, rw, gain, rhalf, rbuf,
+    xf, xo, psum, rsbuf, myscl, scal, scal_o, tr, sb, rawsb, rraw, big, rw, gain, rhalf, rbuf,
     isem, lsem, osem, dsem_s, dsem_r, rs_s, rs_r, ag_s, ag_r, fw_s, fw_r, bk_s, bk_r,
-    rt_s, rt_r,
+    rt_s, rt_r, rw_s, rw_r,
 ):
     srcs, outs, scs = (gate, up, down), (out_g, out_u, out_d), (sc_g, sc_u, sc_d)
     f = lax.axis_index("fsdp")
@@ -130,13 +131,52 @@
 
         lax.fori_loop(0, TILES, one, 0)
 
+    def raw_fill():
+        def one(t, carry):
+            lanes = pl.ds(pl.multiple_of(t * 128, 128), 128)
+            for e in range(HALF):
+                blk = jnp.concatenate([xf[0, e, core, :, lanes], xo[0, e, :, lanes]], axis=0)
+                tr[pl.ds(e, 128, stride=8), :] = blk.T
+            rawsb[pl.ds(t * 128, 128)] = tr[...].reshape(128, 8, 128)
+            return carry
+
+        lax.fori_loop(0, TILES, one, 0)
+
+    def raw_send():
+
+        def go(to):
+            send(rawsb.at[pl.ds(to * PIECE, RAW)], rraw.at[chip, core], rw_s.at[0], rw_r.at[0], to)
+
+        for c in range(2):
+            for dx, dy in OFFS:
+                go(chip_at(dx, dy) * 2 + (core if c == 0 else 1 - core))
+        go(mate)
+
+    def raw_done(scale):
+        rraw[chip, core] = rawsb[pl.ds(f * PIECE, RAW)]
+        await_bytes(rawsb.at[pl.ds(0, 31 * RAW)], rw_r.at[0])
+        inv = 1.0 / scale
+        low = lax.broadcasted_iota(jnp.int32, (8, 128), 1) < 64
+
+        def one(c, carry):
+            lanes = pl.ds(pl.multiple_of(c * 128, 128), 128)
+            for j in range(RAW):
+                p, q = rraw[c, 0, j], rraw[c, 1, j]
+                lo = jnp.where(low, p, q) * inv[:8, j:j + 1]
+                hi = pltpu.roll(jnp.where(low, q, p), 64, 1) * inv[8:, j:j + 1]
+                outs[0][j, :, lanes] = jnp.concatenate([lo, hi], axis=0).astype(BF16)
+            return carry
+
+        lax.fori_loop(0, 16, one, 0)
+
     def bulk(m):
-        n = PIECE // CUT
+        j0 = RAW if m == 0 else 0
+        n = (PIECE - j0) // CUT
 
         def go(to, h):
             send(
-                sb.at[m, pl.ds(to * PIECE + h * n, n)],
-                outs[m].at[pl.ds(h * n, n), pl.ds(pl.multiple_of(core * 8, 8), 8), pl.ds(pl.multiple_of(chip * 128, 128), 128)],
+                sb.at[m, pl.ds(to * PIECE + j0 + h * n, n)],
+                outs[m].at[pl.ds(j0 + h * n, n), pl.ds(pl.multiple_of(core * 8, 8), 8), pl.ds(pl.multiple_of(chip * 128, 128), 128)],
                 bk_s.at[m], bk_r.at[m], to)
 
         def turn(h, carry):
@@ -159,7 +199,7 @@
                 def put(j, carry):
                     outs[m][j, 8 * c:8 * c + 8, lanes] = sb[m, f * PIECE + j]
                     return carry
-                lax.fori_loop(0, PIECE, put, 0)
+                lax.fori_loop(j0, PIECE, put, 0)
 
     def route_pair():
         for c in rin:
@@ -203,7 +243,9 @@
         shift = lax.rem(128 - r, 128)
         a, b = pltpu.roll(a, shift, 1), pltpu.roll(b, shift, 1)
         lane = lax.broadcasted_iota(jnp.int32, (EXP, 128), 1)
-        scs[m][...] = jnp.where(lane < 128 - r, a, b)[:, :PIECE]
+        got = jnp.where(lane < 128 - r, a, b)
+        scs[m][...] = got[:, :PIECE]
+        return got
 
     for m in range(3):
         lax.fori_loop(0, HALF, functools.partial(sums, m), 0)
@@ -213,18 +255,25 @@
         if m == 0:
             swap(0)
     route_pair()
-    for m in range(3):
-        ag_send(m)
+    raw_fill()
+    ag_send(0)
+    raw_send()
+    ag_send(1)
+    ag_send(2)
     route_plane()
     for m in range(3):
         ag_wait(m)
         await_bytes(xo.at[m], dsem_r.at[m])
         fill(m)
         bulk(m)
-    route_line()
-    for m in range(3):
+        if m == 0:
+            route_line()
+    scale = scale_out(0)
+    raw_done(scale)
+    for m in (1, 2):
         scale_out(m)
     route_out()
+    await_bytes(rawsb.at[pl.ds(0, 31 * RAW)], rw_s.at[0])
 
     for m in range(3):
         await_bytes(xo.at[m], dsem_s.at[m])
@@ -235,8 +284,9 @@
     await_bytes(rbuf.at[0, pl.ds(0, 15)], rt_s.at[1])
     await_bytes(rbuf.at[pl.ds(0, 3)], rt_s.at[2])
     for m in range(3):
-        await_bytes(sb.at[m, pl.ds(0, 31 * PIECE)], bk_s.at[m])
-        await_bytes(sb.at[m, pl.ds(0, 31 * PIECE)], bk_r.at[m])
+        size = 31 * (PIECE - RAW if m == 0 else PIECE)
+        await_bytes(sb.at[m, pl.ds(0, size)], bk_s.at[m])
+        await_bytes(sb.at[m, pl.ds(0, size)], bk_r.at[m])
 
 
 def settle(*refs):
@@ -273,12 +323,14 @@
             pltpu.VMEM((3, HALF, TILES + 1, 1, 128), F32),
             pltpu.VMEM((1024, 128), F32),
             pltpu.VMEM((3, COLS, 8, 128), BF16),
+            pltpu.VMEM((COLS, 8, 128), F32),
+            pltpu.VMEM((16, 2, RAW, 8, 128), F32),
             pltpu.VMEM((EXP, (TILES + 1) * 128), F32),
             pltpu.VMEM((EXP, ROWS), F32),
             pltpu.VMEM((1, ROWS), F32),
             pltpu.VMEM((2, EXP, 128), F32),
             pltpu.VMEM((NZ, 16, EXP, 128), BF16),
-            dma((2,)), dma((3, HALF)), dma((3, HALF)), *[dma((3,))] * 12,
+            dma((2,)), dma((3, HALF)), dma((3, HALF)), *[dma((3,))] * 12, dma((1,)), dma((1,)),
         ],
         compiler_params=pltpu.CompilerParams(
             collective_id=0, has_side_effects=True, vmem_limit_bytes=44 * 1024 * 1024

time: 121 us -> 119 us (0.983)
    pallas_call x1, Pallas kernels: 115 us -> 113 us  [body(): pl.pallas_call(exchange, out_shape=shapes, in_specs=[hbm] * 5, out_specs=...]
where the time goes in v2:
time: 119 us
  Pallas kernels  117 us (98%)
  local copies, waits for them, and re-layouts  1.34 us (1%)
    pallas_call x1, Pallas kernels, body(): pl.pallas_call(exchange, out_shape=shapes, in_specs=[hbm] * 5, out_specs=...  113 us
    pallas_call x1, Pallas kernels, body(): pl.pallas_call(settle, out_shape=shapes, in_specs=[vmem] * 7, out_specs=[...  3.55 us

profile of v2, /device:TPU:1, one launch (start us, length us, event | category | flops | bytes accessed | tf_op | source)
XLA Modules:
  0.0 118.8 jit_solution(3051874926436971051)
XLA Ops:
  0.6 0.0 copy-start
  0.6 0.7 copy-done
  1.3 0.0 copy-start.1
  1.3 0.7 copy-done.1
  2.0 113.3 %exchange.1 = (bf16[44,16,2048]{2,1,0:T(8,128)(2,1)S(1)}, bf16[44,16,2048]{2,1,0:T(8,128)(2,1)S(1)}, bf16[44,16,2048]{2,1,0:T(8,128)(2,1)S(1)}, f32[16,44]{1,0:T...) custom-call(f32[16,64,1408]{2,1,0:T(8,128)} %gate.1, f32[16,64,1408]{2,1,0:T(8,128)} %up.1, ...), custom_call_target="tpu_custom_call" | custom-call | tf_op jit(solution)/shard_map/exchange/pallas_call | solution.py:311
  115.3 3.5 %settle.1 = (bf16[44,16,2048]{2,1,0:T(8,128)(2,1)}, bf16[44,16,2048]{2,1,0:T(8,128)(2,1)}, bf16[44,16,2048]{2,1,0:T(8,128)(2,1)}, f32[16,44]{1,0:T(8,128)}, f32[...) custom-call(bf16[44,16,2048]{2,1,0:T(8,128)(2,1)S(1)} %get-tuple-element.21.refs_0_, ...), custom_call_target="tpu_custom_call" | custom-call | tf_op jit(solution)/shard_map/settle/pallas_call | solution.py:340
Async XLA Ops:
  0.6 0.7 copy-start
  1.3 0.7 copy-start.1
